TPU v7x, 128 devices: a whole 4x4x4 slice. The times are simulated.
128 devices in a mesh: grp: 8 (over z, core), col: 16 (over x, y).
Axes of the slice: x: 4, y: 4, z: 4, core: 2. Of those that a mesh axis runs over, the one named last changes fastest.
Arguments:
- x_blocks: bfloat16 [32, 16, 6, 256, 256], P('grp', 'col'), may hold values from -6 to 6
- columns: int32 [32, 16, 6], replicated, may hold values from -1 to 511, as said below
- filter_ids: int32 [32, 16, 6], replicated, may hold values from 0 to 511, as said below
Outputs:
- sign_step: bfloat16 [32, 16, 6, 256, 256], P('grp', 'col')
Inputs may be any that keep to these rules, and one draw needn't show every extreme that they name: `columns`: in each block row of the grid, slot 0 holds the row's own id; the other used slots hold distinct ids of block rows at most one step away along each grid dimension, with periodic wrap; used slots come first, then -1; at least 3 slots are used. `filter_ids`: in each block row, slot 0 holds the row's own id and the others distinct ids of block rows at most one step away along each grid dimension, with periodic wrap.
All inputs are finite; a program needn't handle non-finite values.
Results may differ from a plain program's by a relative error of at most 0.0019.
Values may be sent and summed in bfloat16 or wider, within the bound.
A program may use at most 128 MiB of HBM per device.

v0:
```python
import functools

import jax
import jax.numpy as jnp
from jax import lax
from jax.experimental import pallas as pl
from jax.experimental.pallas import tpu as pltpu
from jax.sharding import PartitionSpec as P

B = 256
KB = 6
KF = 6
RA = 4
OWN = RA * KB
CR = 2 * RA + 2
COLN = CR * KB
ZERO = COLN
FIRST = 5
LATE = 3
RELAY = 4
LEVELS = ((11, 13), (12, 13), (11, 14), (12, 14), (13, 15), (15, 18))

PICKS = OWN * KB
MESH = pl.DeviceIdType.MESH


def padded(cells, sides, width):
    for axis, dim in sides:
        count = lax.axis_size(axis)
        head = lax.slice_in_dim(cells, 0, width, axis=dim)
        tail = lax.slice_in_dim(cells, cells.shape[dim] - width, cells.shape[dim], axis=dim)
        cells = jnp.concatenate(
            [
                lax.ppermute(tail, axis, [(i, (i + 1) % count) for i in range(count)]),
                cells,
                lax.ppermute(head, axis, [((i + 1) % count, i) for i in range(count)]),
            ],
            axis=dim,
        )
    return cells


def block_terms(
    halo, pos_a, pos_c, row_ids, row_cols, left_blocks, stored_table, wanted, grid_a, grid_c
):
    slot_count = halo.shape[2]
    width = halo.shape[3]
    in_use = row_cols >= 0
    source = jnp.where(in_use, row_cols, 0)
    home_a = row_ids // grid_c
    home_c = row_ids % grid_c
    step_a = (source // grid_c - home_a[:, None] + 1) % grid_a - 1
    step_c = (source % grid_c - home_c[:, None] + 1) % grid_c - 1
    place = (pos_a[:, None] + step_a) * halo.shape[1] + pos_c[:, None] + step_c
    flat = halo.reshape((halo.shape[0] * halo.shape[1] * slot_count, width, width))
    stored = stored_table[source]
    matches = stored[:, :, None, :] == wanted[:, None, :, None]
    present = jnp.any(matches, axis=3) & (wanted[:, None, :] >= 0) & in_use[:, :, None]
    slot_of = jnp.argmax(matches.astype(jnp.int32), axis=3)
    block_index = place[:, :, None] * slot_count + slot_of

    def one_row(inputs):
        index_row, present_row, left_row = inputs
        picked = flat[index_row]
        picked = jnp.where(present_row[:, :, None, None], picked, jnp.zeros((), picked.dtype))
        return jnp.einsum("kab,kfbc->fac", left_row, picked, preferred_element_type=jnp.float32)

    return lax.map(one_row, (block_index, present, left_blocks))


def dense(x_blocks, columns, filter_ids):
    grp_count = lax.axis_size("grp")
    col_count = lax.axis_size("col")
    rows_a = x_blocks.shape[0]
    rows_c = x_blocks.shape[1]
    grid_a = rows_a * grp_count
    grid_c = rows_c * col_count
    col_table = columns.reshape(grid_a * grid_c, KB)
    filt_table = filter_ids.reshape(grid_a * grid_c, KF)
    local_rows = rows_a * rows_c
    offsets = jnp.arange(local_rows, dtype=jnp.int32)
    local_a = offsets // rows_c
    local_c = offsets % rows_c
    row_ids = (
        (lax.axis_index("grp") * rows_a + local_a) * grid_c
        + lax.axis_index("col") * rows_c
        + local_c
    )
    row_cols = col_table[row_ids]
    left_blocks = x_blocks.reshape(local_rows, KB, B, B)
    along_col = padded(x_blocks, (("col", 1),), 1)
    near_x = padded(along_col, (("grp", 0),), 1)
    square = block_terms(
        near_x,
        local_a + 1,
        local_c + 1,
        row_ids,
        row_cols,
        left_blocks,
        col_table,
        filt_table[row_ids],
        grid_a,
        grid_c,
    ).astype(jnp.bfloat16)
    square = square.reshape(rows_a, rows_c, KF, B, B)
    square_along = padded(square, (("col", 1),), 1)
    near_square = padded(square_along, (("grp", 0),), 1)
    cubed = block_terms(
        near_square,
        local_a + 1,
        local_c + 1,
        row_ids,
        row_cols,
        left_blocks,
        filt_table,
        row_cols,
        grid_a,
        grid_c,
    )
    in_use = (row_cols >= 0).astype(jnp.float32)
    result = (1.5 * left_blocks.astype(jnp.float32) - cubed * (0.5 / (KB * B))) * in_use[
        :, :, None, None
    ]
    return result.astype(jnp.bfloat16).reshape(x_blocks.shape)


LANES = 128
LISTS = 8
CODE_AT = 0
NEAR_AT = 48
SRC_AT = 96
TABLE_ROWS = 16


def index_kernel(cols_ref, filt_ref, table_ref, level_ref, own_ref, halo_ref, move_ref,
                 cols_s, filt_s):
    grp = lax.axis_index("grp")
    col = lax.axis_index("col")
    core = lax.rem(grp, 2)
    grid_c = cols_ref.shape[1]
    grid_a = cols_ref.shape[2]
    chip = 2 * RA

    def lanes_of(x):
        return jnp.concatenate([x] * (LANES // grid_a), axis=1)

    stored, kept = [], []
    for m in range(KB):
        stored.append(lanes_of(cols_ref[m]))
        kept.append(lanes_of(filt_ref[m]))
        cols_s[m] = stored[m]
        filt_s[m] = kept[m]
    shape = (grid_c, LANES)
    lane = lax.broadcasted_iota(jnp.int32, shape, 1)
    ids = lax.rem(lane, grid_a) * grid_c + lax.broadcasted_iota(jnp.int32, shape, 0)
    in_chip = lax.rem(lane, chip)
    first, last = in_chip == 0, in_chip == chip - 1
    false = jnp.zeros(shape, jnp.int32)

    def either(tests):
        got = tests[0]
        for t in tests[1:]:
            got = got | t
        return got

    totals = []
    for d, step_c in enumerate((1, -1)):
        cols_c = [jnp.roll(x, -step_c, 0) for x in stored]
        filt_c = [jnp.roll(x, -step_c, 0) for x in kept]
        found = []
        for step_a in (-1, 0, 1):
            shift = (-step_a) % LANES
            cols_r = [pltpu.roll(x, shift, 1) if shift else x for x in cols_c]
            filt_r = [pltpu.roll(x, shift, 1) if shift else x for x in filt_c]
            member = either([x == ids for x in cols_r])
            one = [either([stored[m] == x for x in filt_r]) & member & (stored[m] >= 0) for m in range(KB)]
            two = [either([kept[m] == x for x in cols_r]) & member for m in range(KB)]
            found.append((one, two))
        up, mid, down = found
        for phase in (0, 1):
            own_row, halo_row = false, false
            flags = []
            for m in range(KB):
                u, c, w = up[phase][m], mid[phase][m], down[phase][m]
                own = (c | (u & ~first) | (w & ~last)).astype(jnp.int32)
                halo = ((u & first) | (w & last)).astype(jnp.int32)
                flags.append((own, halo))
                own_row = own_row + own
                halo_row = halo_row + halo
            totals.append((phase, d, flags, own_row, halo_row))

    def summed(x, rule):
        at = lax.broadcasted_iota(jnp.int32, (LANES, LANES), 0)
        to = lax.broadcasted_iota(jnp.int32, (LANES, LANES), 1)
        weight = rule(at, to).astype(jnp.float32).astype(jnp.bfloat16)
        return jnp.dot(
            x.astype(jnp.float32).astype(jnp.bfloat16), weight, preferred_element_type=jnp.float32
        ).astype(jnp.int32)

    def same_chip(at, to):
        return (at // chip == lax.rem(to, grid_a) // chip) & (at < grid_a)

    def beside(at, to):
        z = lax.rem(to, grid_a) // chip * chip
        above = lax.rem(z + grid_a - 1, grid_a)
        below = lax.rem(z + chip, grid_a)
        return (at == above) | (at == below)

    def stack(xs):
        return jnp.concatenate(xs, axis=0)

    loads = summed(stack([t[3] for t in totals]), same_chip) + summed(
        stack([t[4] for t in totals]), beside
    )

    def across(x):
        return jnp.where(last, pltpu.roll(x, LANES - 1, 1), pltpu.roll(x, 1, 1))

    kept_own, kept_halo, got0, got1 = [], [], [], []
    for p, (phase, d, flags, _, _) in enumerate(totals):
        load = loads[p * grid_c : (p + 1) * grid_c]
        lead = jnp.where(last, load - across(load), across(load) - load)
        far = jnp.abs(lead)
        count = jnp.zeros(shape, jnp.int32)
        for step in range(RELAY):
            count = count + (far >= 3 * step + 2).astype(jnp.int32)
        ups = (lead > 0).astype(jnp.int32)
        rim = (first | last).astype(jnp.int32)
        both = [own * halo * rim for own, halo in flags]
        lower = [jnp.where(last, own, halo) for own, halo in flags]
        upper = [jnp.where(last, halo, own) for own, halo in flags]
        single = [
            jnp.where(ups > 0, lower[m], upper[m]) * rim - both[m] for m in range(KB)
        ]
        n_both = sum(both[1:], both[0])
        n_single = sum(single[1:], single[0])
        both_rank = jnp.where(last, 0, across(n_both))
        single_rank = n_both + across(n_both) + jnp.where(last, 0, across(n_single))
        own_row, halo_row, moved_row = false, false, false
        for m in range(KB):
            rank = jnp.where(both[m] > 0, both_rank, single_rank)
            moved = ((both[m] + single[m]) > 0) & (rank < count)
            move = jnp.where(moved, rank + 1 + 8 * ups, 0)
            both_rank = both_rank + both[m]
            single_rank = single_rank + single[m]
            own = jnp.where(moved, 0, flags[m][0])
            halo = jnp.where(moved, 0, flags[m][1])
            own_ref[phase, d, m] = own
            halo_ref[phase, d, m] = halo
            move_ref[phase, d, m] = move
            own_row, halo_row = own_row + own, halo_row + halo
            moved_row = moved_row + moved.astype(jnp.int32)
        moved_row = moved_row + across(moved_row)
        kept_own.append(own_row)
        kept_halo.append(halo_row)
        got0.append(jnp.where(first, moved_row * ups, 0))
        got1.append(jnp.where(last, moved_row * (1 - ups), 0))

    def split(n0, n1, total, extra0, extra1):
        half = jnp.clip((total + extra1 - extra0 + 1) >> 1, 0, total)
        return half, jnp.maximum(FIRST - n0, 0), jnp.maximum(FIRST - n1, 0)

    own_all = stack(kept_own)
    n0 = summed(own_all, lambda at, to: same_chip(at, to) & (lax.rem(at, chip) < RA))
    n1 = summed(own_all, lambda at, to: same_chip(at, to) & (lax.rem(at, chip) >= RA))
    total = n0 + n1 + summed(stack(kept_halo), beside)
    extra0 = summed(stack(got0), same_chip)
    extra1 = summed(stack(got1), same_chip)
    half, gap0, gap1 = split(n0, n1, total, extra0, extra1)
    rest = total - half
    fill = jnp.maximum(
        half + jnp.where(half > n0, gap0, 0) + extra0,
        rest + jnp.where(rest > n1, gap1, 0) + extra1,
    )
    most = [jnp.int32(FIRST + RELAY), jnp.int32(FIRST + RELAY)]
    for p, (phase, _, _, _, _) in enumerate(totals):
        most[phase] = jnp.maximum(most[phase], jnp.max(fill[p * grid_c : (p + 1) * grid_c]))
    level = jnp.int32(len(LEVELS))
    for at in reversed(range(len(LEVELS))):
        fits = (most[0] <= LEVELS[at][0]) & (most[1] <= LEVELS[at][1])
        level = jnp.where(fits, at, level)
    level_ref[0] = level

    z = grp // 2
    shift = lax.rem(LANES + 1 - z * chip, LANES)
    west = lax.rem(col + grid_c - 1, grid_c)
    east = lax.rem(col + 1, grid_c)
    row8 = (LISTS, LANES)
    lane8 = lax.broadcasted_iota(jnp.int32, row8, 1)
    rim = (lane8 == 0) | (lane8 == CR - 1)
    lists = [(p, d, c) for p in (0, 1) for d, c in ((0, col), (1, col), (0, west), (1, east))]

    def near(ref_rows):
        return pltpu.roll(jnp.concatenate(ref_rows, axis=0), shift, 1)

    need, in_row, stores, moves = [], [], [], []
    run = jnp.zeros(row8, jnp.int32)
    relayed = jnp.zeros(row8, jnp.int32)
    low_end = lane8 <= 1
    for m in range(KB):
        own = near([own_ref[p, d, m, pl.ds(c, 1), :] for p, d, c in lists])
        halo = near([halo_ref[p, d, m, pl.ds(c, 1), :] for p, d, c in lists])
        flags = jnp.where(lane8 < CR, jnp.where(rim, halo, own), 0)
        need.append(flags)
        in_row.append(run)
        run = run + flags
        move = near([move_ref[p, d, m, pl.ds(c, 1), :] for p, d, c in lists])
        move = jnp.where((lane8 <= 1) | ((lane8 >= CR - 2) & (lane8 < CR)), move, 0)
        mine = (move > 0) & ((move > 8) == low_end)
        moves.append((move, mine))
        relayed = relayed + mine.astype(jnp.int32)
        rows = [cols_s[m, pl.ds(c, 1), :] for c in (west, col, east)]
        rows += [filt_s[m, pl.ds(c, 1), :] for c in (west, col, east)]
        stores.append(near(rows + rows[:2]))
    n0 = summed(run, lambda at, to: (at >= 1) & (at <= RA))
    n1 = summed(run, lambda at, to: (at > RA) & (at <= chip))
    above = summed(run, lambda at, to: at == 0)
    below = summed(run, lambda at, to: at == CR - 1)
    ahead = summed(
        run, lambda at, to: (at < to) & (((at >= 1) & (to <= RA)) | ((at > RA) & (to <= chip)))
    )
    total = n0 + n1 + above + below
    extra0 = summed(relayed, lambda at, to: at <= 1)
    extra1 = summed(relayed, lambda at, to: at > 1)
    half, gap0, gap1 = split(n0, n1, total, extra0, extra1)
    east_list = lax.rem(lax.broadcasted_iota(jnp.int32, row8, 0), 4) == 3
    of0 = (lane8 >= 1) & (lane8 <= RA)
    of1 = (lane8 > RA) & (lane8 <= chip)
    slots = lax.broadcasted_iota(jnp.int32, (32, LANES), 0) + core * 32
    entry = lax.broadcasted_iota(jnp.int32, (32, LANES), 1) * KB
    source = [jnp.zeros((32, LANES), jnp.int32) for _ in range(4)]
    codes = []
    for m in range(KB):
        place = ahead + in_row[m]
        place = jnp.where(lane8 == 0, n0 + in_row[m], place)
        place = jnp.where(lane8 == CR - 1, n0 + above + in_row[m], place)
        place = jnp.where(of1, total - 1 - place, place)
        turned = total - 1 - place
        slot0 = place + jnp.where(of0, 0, gap0)
        slot1 = turned + jnp.where(of1, 0, gap1)
        slot0 = slot0 + jnp.where(slot0 >= FIRST, extra0, 0)
        slot1 = slot1 + jnp.where(slot1 >= FIRST, extra1, 0)
        code = jnp.where(place < half, slot0, 32 + slot1)
        move, mine = moves[m]
        rank = (move & 7) - 1
        code = jnp.where(mine, jnp.where(low_end, FIRST, 32 + FIRST) + rank, code)
        code = jnp.where((move > 0) & ~mine, jnp.where(east_list, 96, 128) + rank, code)
        codes.append(code)
        sent = jnp.where((need[m] > 0) | mine, code, -1)
        for i, at in enumerate((0, 1, 4, 5)):
            same = jnp.broadcast_to(sent[at : at + 1], (32, LANES)) == slots
            source[i] = source[i] + jnp.where(same, entry + m, 0)
    lane32 = lax.broadcasted_iota(jnp.int32, (32, LANES), 1)
    out = jnp.zeros((32, LANES), jnp.int32)
    for i in range(4):
        out = jnp.where(lane32 == i, jnp.sum(source[i], axis=1, keepdims=True), out)
    table_ref[...] = jnp.concatenate(codes + stores + [out], axis=0).T[:TABLE_ROWS]


def list_tables(columns, filter_ids):
    grid_a, grid_c, _ = columns.shape
    ints = lambda *shape: pltpu.VMEM(shape, jnp.int32)
    return pl.pallas_call(
        index_kernel,
        out_shape=(
            jax.ShapeDtypeStruct((TABLE_ROWS, LANES), jnp.int32),
            jax.ShapeDtypeStruct((1,), jnp.int32),
        ),
        in_specs=[pl.BlockSpec(memory_space=pltpu.VMEM)] * 2,
        out_specs=(
            pl.BlockSpec(memory_space=pltpu.VMEM),
            pl.BlockSpec(memory_space=pltpu.SMEM),
        ),
        scratch_shapes=[
            ints(2, 2, KB, grid_c, LANES), ints(2, 2, KB, grid_c, LANES),
            ints(2, 2, KB, grid_c, LANES),
            ints(KB, grid_c, LANES), ints(KF, grid_c, LANES),
        ],
        name="block_lists",
    )(columns.transpose(2, 1, 0), filter_ids.transpose(2, 1, 0))


def kernel(q1, q2, grid_a, grid_c, grp_count, col_count, tab, x_hbm, out_ref, acc_ref, late, xv, todo, pick, colp1, rcv1, snd1, colp2, rcv2,
           snd2, sown, lsem, zsem, hs1, hr1, fs1, fr1, hs2, hr2, fs2, fr2, lr2, ysem):
    grp = lax.axis_index("grp")
    col = lax.axis_index("col")
    core = lax.rem(grp, 2)
    partner = (grp + 1 - 2 * core, col)
    zpeer = (lax.rem(grp + grp_count - 1 + 2 * core, grp_count), col)
    right = (grp, lax.rem(col + 1, col_count))
    left = (grp, lax.rem(col + col_count - 1, col_count))
    own0 = (1 + RA * core) * KB
    zout = (RA - 1) * core * KB
    zdst = (CR - 1) * (1 - core) * KB
    zin = (CR - 1) * core * KB

    to_xv = pltpu.make_async_copy(x_hbm, xv, lsem.at[0])
    to_col = pltpu.make_async_copy(x_hbm, colp1.at[pl.ds(own0, OWN)], lsem.at[1])
    to_xv.start()

    barrier = pltpu.get_barrier_semaphore()
    for peer in (partner, zpeer, right, left):
        pl.semaphore_signal(barrier, inc=1, device_id=peer, device_id_type=MESH)
    pl.semaphore_wait(barrier, 4)

    def remote(src, dst, send, recv, device):
        return pltpu.make_async_remote_copy(
            src_ref=src, dst_ref=dst, send_sem=send, recv_sem=recv,
            device_id=device, device_id_type=MESH,
        )

    def zsend(src, colp, p):
        return remote(src.at[pl.ds(zout, KB)], colp.at[pl.ds(zdst, KB)],
                      zsem.at[p, 0], zsem.at[p, 1], zpeer)

    def zfwd(colp, p):
        here = colp.at[pl.ds(zin, KB)]
        return remote(here, here, zsem.at[p, 2], zsem.at[p, 3], partner)

    def share(src, colp, p):
        return remote(src, colp.at[pl.ds(own0, OWN)], zsem.at[p, 4], zsem.at[p, 5], partner)

    def hop(snd, rcv, hs, hr, q, d, s):
        return remote(snd.at[d, s], rcv.at[(2 * d + core) * q + s], hs, hr.at[s],
                      (right, left)[d])

    def fwd(rcv, fs, fr, q, d, s):
        here = rcv.at[(2 * d + core) * q + s]
        return remote(here, here, fs, fr, partner)

    def late_hop(d, i):
        s = q2 - LATE + i
        return remote(snd2.at[d, s], late.at[(2 * d + core) * LATE + i], hs2, hr2.at[s],
                      (right, left)[d])

    def late_fwd(d, i):
        here = late.at[(2 * d + core) * LATE + i]
        return remote(here, here, fs2, lr2, partner)

    def relay(rcv, p, q, d, s):
        rank = s - FIRST
        return remote(rcv.at[(2 * d + core) * q + s], rcv.at[4 * q + d * RELAY + rank],
                      ysem.at[p, 0], ysem.at[p, 1], zpeer)

    def wait_all(like, sem):
        pltpu.make_async_copy(like, like, sem).wait()

    def right_factor(colp, rcv, q, v):
        is_col = v < 64
        at_col = jnp.where(is_col, v, ZERO)
        at_rcv = jnp.where(is_col, 0, v - 64)
        part = at_rcv >> 5
        slot = at_rcv & 31
        direct = jnp.minimum(part, 3) * q + jnp.minimum(slot, q - 1)
        passed = 4 * q + jnp.clip((part - 4) * RELAY + slot, 0, 2 * RELAY - 1)
        return jnp.where(is_col, colp[at_col], rcv[jnp.where(part < 4, direct, passed)])

    def product(colp, rcv, phase, row, entry):
        acc = None
        for k in range(KB):
            v = pick[phase * PICKS + entry * KB + k]
            term = jnp.dot(xv[row * KB + k], right_factor(colp, rcv, (q1, q2 - LATE)[phase], v),
                           preferred_element_type=jnp.float32)
            acc = term if acc is None else acc + term
        return acc

    def sent(phase, d, s):
        return tab[2 * phase + d, SRC_AT + s]

    def list_entry(phase, d, s):
        return jnp.clip(sent(phase, d, s) - own0, 0, OWN - 1)

    def find_factors(at):
        row = at // KB
        k = at - KB * row
        here = 1 + RA * core + row
        source = tab[here, NEAR_AT + 8 * k + 1]
        in_use = source >= 0
        source = jnp.where(in_use, source, 0)
        step_a = lax.rem(source // grid_c - (grp * RA + row) + 1 + grid_a, grid_a) - 1
        side = lax.rem(lax.rem(source, grid_c) - col + 1 + grid_c, grid_c)
        step_a = jnp.where(in_use, jnp.clip(step_a, -1, 1), 0)
        side = jnp.where(in_use, jnp.minimum(side, 2), 1)
        there = here + step_a
        mark_row = lax.broadcasted_iota(jnp.int32, (8, LANES), 0)
        there_at = lax.broadcasted_iota(jnp.int32, (8, LANES), 1) == at
        marks = todo[...]
        for phase in range(2):
            held, spot = [], []
            for m in range(KB):
                held.append(tab[there, NEAR_AT + 8 * m + side + 3 * phase])
                code = tab[there, CODE_AT + 8 * m + 4 * phase + jnp.where(side == 0, 2, 3)]
                far = code + jnp.where(side == 0, 64, 128)
                spot.append(jnp.where(side == 1, there * KB + m, far))
            for f in range(KF):
                wanted = tab[here, NEAR_AT + 8 * f + 1 + 3 * (1 - phase)]
                usable = in_use & (wanted >= 0)
                got = jnp.int32(ZERO)
                for m in range(KB):
                    got = jnp.where(held[m] == wanted, spot[m], got)
                got = jnp.where(usable, got, ZERO)
                if phase:
                    part, slot = (got - 64) >> 5, (got - 64) & 31
                    waits = (got >= 64) & (part < 4) & (slot >= q2 - LATE)
                    code = jnp.clip(part * LATE + slot - (q2 - LATE), 0, 4 * LATE - 1)
                    marks = jnp.where(there_at & (mark_row == f), jnp.where(waits, code, -1), marks)
                    got = jnp.where(waits, ZERO, got)
                pick[phase * PICKS + (row * KB + f) * KB + k] = got
        todo[...] = marks

    zero = jnp.zeros((B, B), jnp.bfloat16)

    zs1, zf1, sh1 = zsend(xv, colp1, 0), zfwd(colp1, 0), share(xv, colp1, 0)
    to_xv.wait()
    zs1.start()
    to_col.start()
    sh1.start()
    hop1 = functools.partial(hop, snd1, rcv1, hs1, hr1, q1)
    fwd1 = functools.partial(fwd, rcv1, fs1, fr1, q1)
    pass1 = functools.partial(relay, rcv1, 0, q1)

    @pl.loop(0, FIRST)
    def _(s):
        for d in range(2):
            snd1[d, s] = xv[list_entry(0, d, s)]

        @pl.when(s > 0)
        def _():
            for d in range(2):
                hop1(d, s - 1).start()

    colp1[ZERO] = zero
    colp2[ZERO] = zero
    for d in range(2):
        hop1(d, FIRST - 1).start()
    to_col.wait()
    zs1.wait_recv()
    zf1.start()
    sh1.wait_recv()
    zf1.wait_recv()

    @pl.loop(FIRST, q1)
    def _(s):
        for d in range(2):
            snd1[d, s] = colp1[sent(0, d, s)]

        @pl.when(s > FIRST)
        def _():
            for d in range(2):
                hop1(d, s - 1).start()

    for d in range(2):
        hop1(d, q1 - 1).start()

    todo[...] = jnp.full((8, LANES), -1, jnp.int32)
    pl.loop(0, OWN)(find_factors)

    @pl.loop(0, q1)
    def _(s):
        wait_all(rcv1.at[pl.ds(0, 2)], hr1.at[s])
        for d in range(2):
            fwd1(d, s).start()

        @pl.when((s >= FIRST) & (s < FIRST + RELAY))
        def _():
            for d in range(2):
                pass1(d, s).start()

    wait_all(snd1, fr1)
    wait_all(rcv1.at[pl.ds(0, 2 * RELAY)], ysem.at[0, 1])

    zs2, zf2, sh2 = zsend(sown, colp2, 1), zfwd(colp2, 1), share(sown, colp2, 1)
    hop2 = functools.partial(hop, snd2, rcv2, hs2, hr2, q2 - LATE)
    fwd2 = functools.partial(fwd, rcv2, fs2, fr2, q2 - LATE)
    pass2 = functools.partial(relay, rcv2, 1, q2 - LATE)

    @pl.loop(0, 2 + OWN // 2)
    def _(t):
        listed = t < 2
        slot = jnp.where(listed, t, 0)
        at = jnp.where(listed, 0, t - 2)
        step = at // 3
        row = step + core * (RA - 1 - 2 * step)
        for d in range(2):
            own_entry = row * KB + (at - 3 * step) * 2 + d
            entry = jnp.where(listed, list_entry(1, d, slot), own_entry)
            block = product(colp1, rcv1, 0, entry // KB, entry).astype(jnp.bfloat16)

            @pl.when(listed)
            def _():
                snd2[d, slot] = block

            @pl.when(~listed)
            def _():
                sown[own_entry] = block
                colp2[own0 + own_entry] = block

        @pl.when(listed)
        def _():
            hop2(0, slot).start()

        @pl.when((t > 0) & (t < 3))
        def _():
            hop2(1, t - 1).start()

        @pl.when(t == 5)
        def _():
            zs2.start()

    @pl.loop(2, FIRST)
    def _(s):
        for d in range(2):
            snd2[d, s] = sown[list_entry(1, d, s)]

        @pl.when(s > 2)
        def _():
            for d in range(2):
                hop2(d, s - 1).start()

    sh2.start()
    for d in range(2):
        hop2(d, FIRST - 1).start()
    zs2.wait_recv()
    zf2.start()
    sh2.wait_recv()
    zf2.wait_recv()

    @pl.loop(FIRST, q2 - LATE)
    def _(s):
        for d in range(2):
            snd2[d, s] = colp2[sent(1, d, s)]

        @pl.when(s > FIRST)
        def _():
            for d in range(2):
                hop2(d, s - 1).start()

    for i in range(LATE):
        s = q2 - LATE + i
        for d in range(2):
            snd2[d, s] = colp2[sent(1, d, s)]
        for d in range(2):
            (late_hop(d, i - 1) if i else hop2(d, s - 1)).start()
    for d in range(2):
        late_hop(d, LATE - 1).start()

    @pl.loop(0, q2 - LATE)
    def _(s):
        wait_all(rcv2.at[pl.ds(0, 2)], hr2.at[s])
        for d in range(2):
            fwd2(d, s).start()

        @pl.when((s >= FIRST) & (s < FIRST + RELAY))
        def _():
            for d in range(2):
                pass2(d, s).start()

    wait_all(rcv2.at[pl.ds(0, 2 * (q2 - LATE))], fr2)
    wait_all(rcv2.at[pl.ds(0, 2 * RELAY)], ysem.at[1, 1])

    def pass_late(i):
        wait_all(rcv2.at[pl.ds(0, 2)], hr2.at[q2 - LATE + i])
        for d in range(2):
            late_fwd(d, i).start()

    @pl.loop(0, OWN // 2)
    def _(t):
        row = t // 3
        for u in range(2):
            entry = 2 * t + u
            cubed = product(colp2, rcv2, 1, row, entry)
            in_use = tab[1 + RA * core + row, NEAR_AT + 8 * (entry - row * KB) + 1] >= 0
            own = xv[entry].astype(jnp.float32)
            step = 1.5 * own - cubed * (0.5 / (KB * B))
            out_ref[entry] = jnp.where(in_use, step, 0.0).astype(jnp.bfloat16)
            acc_ref[entry] = cubed

        for i, when in enumerate((5, 11)):

            @pl.when(t == when)
            def _():
                pass_late(i)

    pass_late(2)

    wait_all(late.at[pl.ds(0, 2 * LATE)], lr2)
    zs1.wait_send()
    zf1.wait_send()
    sh1.wait_send()
    zs2.wait_send()
    zf2.wait_send()
    sh2.wait_send()
    for snd, rcv, hs, fs, p in ((snd1, rcv1, hs1, fs1, 0), (snd2, rcv2, hs2, fs2, 1)):
        wait_all(snd, hs)
        wait_all(snd, fs)
        wait_all(rcv.at[pl.ds(0, 2 * RELAY)], ysem.at[p, 0])


def sparse(level, grid_a, grid_c, x_blocks, table):
    q1, q2 = LEVELS[level]
    blocks = x_blocks.reshape(OWN, B, B)
    vm = lambda *lead: pltpu.VMEM((*lead, B, B), jnp.bfloat16)
    dma = lambda *lead: pltpu.SemaphoreType.DMA(lead)
    held = OWN + 2 * COLN + 2 + 6 * (q1 + q2) + 4 * RELAY + 16
    out, acc, late, xv, todo = pl.pallas_call(
        functools.partial(kernel, q1, q2, grid_a, grid_c, lax.axis_size("grp"), lax.axis_size("col")),
        out_shape=(
            pltpu.VMEM(blocks.shape, jnp.bfloat16),
            pltpu.VMEM(blocks.shape, jnp.float32),
            pltpu.VMEM((4 * LATE, B, B), jnp.bfloat16),
            pltpu.VMEM(blocks.shape, jnp.bfloat16),
            pltpu.VMEM((8, LANES), jnp.int32),
        ),
        in_specs=[
            pl.BlockSpec(memory_space=pltpu.SMEM),
            pl.BlockSpec(memory_space=pl.ANY),
        ],
        out_specs=tuple(pl.BlockSpec(memory_space=pltpu.VMEM) for _ in range(5)),
        scratch_shapes=[
            pltpu.SMEM((2 * PICKS,), jnp.int32),
            vm(COLN + 1), vm(4 * q1 + 2 * RELAY), vm(2, q1), vm(COLN + 1),
            vm(4 * (q2 - LATE) + 2 * RELAY), vm(2, q2), vm(OWN),
            dma(2), dma(2, 6),
            dma(), dma(q1), dma(), dma(), dma(), dma(q2), dma(), dma(), dma(), dma(2, 2),
        ],
        compiler_params=pltpu.CompilerParams(
            collective_id=level, has_side_effects=True, vmem_limit_bytes=held * B * B * 2
        ),
        name=f"sign_step_{q1}_{q2}",
    )(table, blocks)
    return finished(todo, out, acc, late, xv).reshape(x_blocks.shape)


def finish_kernel(todo, out_ref, acc_ref, late, xv, res, some, total, fixed, sem):
    def write(src, entry):
        return pltpu.make_async_copy(src.at[entry], res.at[entry], sem)

    @pl.loop(0, KF)
    def _(f):
        for row in range(RA):
            entry = row * KB + f
            latest = todo[f, row * KB]
            for k in range(1, KB):
                latest = jnp.maximum(latest, todo[f, row * KB + k])
            some[entry] = latest

            @pl.when(latest < 0)
            def _():
                write(out_ref, entry).start()

    @pl.loop(0, OWN)
    def _(entry):
        @pl.when(some[entry] >= 0)
        def _():
            row, f = entry // KB, entry % KB
            total[...] = acc_ref[entry]
            for k in range(KB):
                code = todo[f, row * KB + k]

                @pl.when(code >= 0)
                def _():
                    total[...] += jnp.dot(
                        xv[row * KB + k],
                        late[jnp.clip(code, 0, 4 * LATE - 1)],
                        preferred_element_type=jnp.float32,
                    )

            own = xv[entry].astype(jnp.float32)
            fixed[entry] = (1.5 * own - total[...] * (0.5 / (KB * B))).astype(jnp.bfloat16)

    @pl.loop(0, OWN)
    def _(entry):
        @pl.when(some[entry] >= 0)
        def _():
            write(fixed, entry).start()

    pltpu.make_async_copy(out_ref, res, sem).wait()


def finished(todo, out, acc, late, xv):
    return pl.pallas_call(
        finish_kernel,
        out_shape=jax.ShapeDtypeStruct(out.shape, out.dtype),
        in_specs=[pl.BlockSpec(memory_space=pltpu.SMEM)]
        + [pl.BlockSpec(memory_space=pltpu.VMEM)] * 4,
        out_specs=pl.BlockSpec(memory_space=pl.ANY),
        scratch_shapes=[
            pltpu.SMEM((OWN,), jnp.int32),
            pltpu.VMEM((B, B), jnp.float32),
            pltpu.VMEM(out.shape, out.dtype),
            pltpu.SemaphoreType.DMA(()),
        ],
        compiler_params=pltpu.CompilerParams(vmem_limit_bytes=20 * 1024 * 1024),
        name="finish",
    )(todo, out, acc, late, xv)


def local(x_blocks, columns, filter_ids):
    grid_a, grid_c, _ = columns.shape
    table, level = list_tables(columns, filter_ids)
    branches = [
        functools.partial(lambda at, x, c, f, t: sparse(at, grid_a, grid_c, x, t), at)
        for at in range(len(LEVELS))
    ]
    branches.append(lambda x, c, f, t: dense(x, c, f))
    return lax.switch(level[0], branches, x_blocks, columns, filter_ids, table)


def solution(mesh):
    return jax.shard_map(
        local,
        mesh=mesh,
        in_specs=(P("grp", "col", None, None, None), P(), P()),
        out_specs=P("grp", "col", None, None, None),
        check_vma=False,
    )
```

profile of v0, /device:TPU:1, one launch (start us, length us, event | category | flops | bytes accessed | tf_op | source)
XLA Modules:
  0.0 107.2 jit_solution(9233248595886086533)
XLA Ops:
  0.0 3.3 %block_lists.1 = (s32[16,128]{1,0:T(8,128)S(1)}, s32[1]{0:T(128)}) custom-call(s32[6,16,32]{2,1,0:T(8,128)} %bitcast.139, s32[6,16,32]{2,1,0:T(8,128)} %bitcast.140), custom_call_target="tpu_custom_call" | custom-call | tf_op jit(solution)/shard_map/block_lists/pallas_call | solution.py:363
  3.9 103.1 %conditional.1 = (bf16[4,1,6,256,256]{4,3,2,1,0:T(8,128)(2,1)}) conditional(s32[]{:T(128)} %bitcast.49, (bf16[4,1,6,256,256]{4,3,2,1,0:T(8,128)(2,1)}, s32[16,128]{1,0:T(8,128)S(1)}) %tuple.37, (bf16[4,1,6,256,256]{4,3,2,1,0:T(8,128)(2,1)}, s32[16,128]{1,0:T(8,128)S(1)}) %tuple.37, ...), branch_computations={%region_0.0_spmd, %region_1.0_spmd, %region_2.0_spmd, %region_3.0_... | conditional | flops 2497731584 | bytes 360377280 | solution.py:806
  3.9 100.2 %sign_step_11_13.1 = (bf16[24,256,256]{2,1,0:T(8,128)(2,1)S(1)}, f32[24,256,256]{2,1,0:T(8,128)S(1)}, bf16[12,256,256]{2,1,0:T(8,128)(2,1)S(1)}, bf16[24,256,256]{2,1,0:T(8,128)(2,1)S(1)}, s32[8,128]{1,0:T(8,128)S(1)}) custom-call(s32[16,128]{1,0:T(8,128)S(1)} %get-tuple-element.78.tab, bf16[24,256,256]{2,1,0:T(8,128)(2,1)} %bitcast.122), custom_call_target="tpu_custom_call" | custom-call | tf_op jit(solution)/shard_map/cond/branch_0_fun/sign_step_11_13/pallas_call | solution.py:705
  104.2 2.6 %finish.6 = bf16[24,256,256]{2,1,0:T(8,128)(2,1)} custom-call(s32[8,128]{1,0:T(8,128)S(1)} %get-tuple-element.87.todo, bf16[24,256,256]{2,1,0:T(8,128)(2,1)S(1)} %get-tuple-element.92.out_ref, f32[24,256,256]{2,1,0:T(8,128)S(1)} %get-tuple-element.94.acc_ref, bf16[12,256,256]{2,1,0:T(8,128)(2,1)S(1)} %get-tuple-element.96.late, ...), custom_call_target="tpu_custom_call" | custom-call | tf_op jit(solution)/shard_map/cond/branch_0_fun/finish/pallas_call | solution.py:781
where the time goes:
time: 107 us
  Pallas kernels  106 us (99%)
    pallas_call x1, Pallas kernels, sparse(): pl.pallas_call(functools.partial(kernel, q1, q2, grid_a, grid_c, lax.axis...  100 us
    pallas_call x1, Pallas kernels, list_tables(): pl.pallas_call(index_kernel, out_shape=(jax.ShapeDtypeStruct((TABLE_ROWS,...  3.25 us
    pallas_call x1, Pallas kernels, finished(): pl.pallas_call(finish_kernel, out_shape=jax.ShapeDtypeStruct(out.shape, o...  2.58 us

commit v1 on v0

--- a/solution.py
+++ b/solution.py
@@ -574,45 +574,44 @@
     fwd2 = functools.partial(fwd, rcv2, fs2, fr2, q2 - LATE)
     pass2 = functools.partial(relay, rcv2, 1, q2 - LATE)
 
-    @pl.loop(0, 2 + OWN // 2)
+    @pl.loop(0, 3 + OWN // 2)
     def _(t):
-        listed = t < 2
-        slot = jnp.where(listed, t, 0)
-        at = jnp.where(listed, 0, t - 2)
+        listed = (t == 0) | (t == 4) | (t == 5)
+        slot = jnp.where(listed, jnp.maximum(t - 3, 0), 0)
+        at = jnp.where(listed, 3, jnp.where(t < 4, t - 1, t - 3))
         step = at // 3
+
+        @pl.when(t == 4)
+        def _():
+            zs2.start()
+
         row = step + core * (RA - 1 - 2 * step)
         for d in range(2):
             own_entry = row * KB + (at - 3 * step) * 2 + d
             entry = jnp.where(listed, list_entry(1, d, slot), own_entry)
             block = product(colp1, rcv1, 0, entry // KB, entry).astype(jnp.bfloat16)
-
-            @pl.when(listed)
-            def _():
-                snd2[d, slot] = block
-
-            @pl.when(~listed)
-            def _():
-                sown[own_entry] = block
-                colp2[own0 + own_entry] = block
+            snd2[d, jnp.where(listed, slot, q2 - 1)] = block
+            sown[own_entry] = block
+            colp2[own0 + own_entry] = block
 
         @pl.when(listed)
         def _():
             hop2(0, slot).start()
 
-        @pl.when((t > 0) & (t < 3))
-        def _():
-            hop2(1, t - 1).start()
-
-        @pl.when(t == 5)
-        def _():
-            zs2.start()
-
-    @pl.loop(2, FIRST)
+        @pl.when(t == 1)
+        def _():
+            hop2(1, 0).start()
+
+        @pl.when((t == 5) | (t == 6))
+        def _():
+            hop2(1, t - 4).start()
+
+    @pl.loop(3, FIRST)
     def _(s):
         for d in range(2):
             snd2[d, s] = sown[list_entry(1, d, s)]
 
-        @pl.when(s > 2)
+        @pl.when(s > 3)
         def _():
             for d in range(2):
                 hop2(d, s - 1).start()

time: 107 us -> 98.4 us (0.920); the launches traced: 107 us -> 96.6 us
  Pallas kernels: 106 us -> 95.5 us
    pallas_call x1, Pallas kernels: 100 us -> 90 us  [sparse(): pl.pallas_call(functools.partial(kernel, q1, q2, grid_a, grid_c, lax.axis...]
where the time goes in v1:
time: 98.4 us; the launch traced here: 96.6 us
  Pallas kernels  95.5 us (97%)
    pallas_call x1, Pallas kernels, sparse(): pl.pallas_call(functools.partial(kernel, q1, q2, grid_a, grid_c, lax.axis...  90 us
    pallas_call x1, Pallas kernels, list_tables(): pl.pallas_call(index_kernel, out_shape=(jax.ShapeDtypeStruct((TABLE_ROWS,...  3.25 us
    pallas_call x1, Pallas kernels, finished(): pl.pallas_call(finish_kernel, out_shape=jax.ShapeDtypeStruct(out.shape, o...  2.26 us

profile of v1, /device:TPU:1, one launch (start us, length us, event | category | flops | bytes accessed | tf_op | source)
XLA Modules:
  0.0 96.6 jit_solution(4219354377008954300)
XLA Ops:
  0.0 3.3 %block_lists.1 = (s32[16,128]{1,0:T(8,128)S(1)}, s32[1]{0:T(128)}) custom-call(s32[6,16,32]{2,1,0:T(8,128)} %bitcast.139, s32[6,16,32]{2,1,0:T(8,128)} %bitcast.140), custom_call_target="tpu_custom_call" | custom-call | tf_op jit(solution)/shard_map/block_lists/pallas_call | solution.py:363
  3.9 92.6 %conditional.1 = (bf16[4,1,6,256,256]{4,3,2,1,0:T(8,128)(2,1)}) conditional(s32[]{:T(128)} %bitcast.49, (bf16[4,1,6,256,256]{4,3,2,1,0:T(8,128)(2,1)}, s32[16,128]{1,0:T(8,128)S(1)}) %tuple.37, (bf16[4,1,6,256,256]{4,3,2,1,0:T(8,128)(2,1)}, s32[16,128]{1,0:T(8,128)S(1)}) %tuple.37, ...), branch_computations={%region_0.0_spmd, %region_1.0_spmd, %region_2.0_spmd, %region_3.0_... | conditional | flops 2497731584 | bytes 360377280 | solution.py:805
  3.9 90.0 %sign_step_11_13.1 = (bf16[24,256,256]{2,1,0:T(8,128)(2,1)S(1)}, f32[24,256,256]{2,1,0:T(8,128)S(1)}, bf16[12,256,256]{2,1,0:T(8,128)(2,1)S(1)}, bf16[24,256,256]{2,1,0:T(8,128)(2,1)S(1)}, s32[8,128]{1,0:T(8,128)S(1)}) custom-call(s32[16,128]{1,0:T(8,128)S(1)} %get-tuple-element.78.tab, bf16[24,256,256]{2,1,0:T(8,128)(2,1)} %bitcast.122), custom_call_target="tpu_custom_call" | custom-call | tf_op jit(solution)/shard_map/cond/branch_0_fun/sign_step_11_13/pallas_call | solution.py:704
  94.0 2.3 %finish.6 = bf16[24,256,256]{2,1,0:T(8,128)(2,1)} custom-call(s32[8,128]{1,0:T(8,128)S(1)} %get-tuple-element.87.todo, bf16[24,256,256]{2,1,0:T(8,128)(2,1)S(1)} %get-tuple-element.92.out_ref, f32[24,256,256]{2,1,0:T(8,128)S(1)} %get-tuple-element.94.acc_ref, bf16[12,256,256]{2,1,0:T(8,128)(2,1)S(1)} %get-tuple-element.96.late, ...), custom_call_target="tpu_custom_call" | custom-call | tf_op jit(solution)/shard_map/cond/branch_0_fun/finish/pallas_call | solution.py:780
